TPU v7x, 32 devices: a whole 2x2x4 slice. The times are simulated.
32 devices in a mesh: dp: 8 (over z, y), ep: 4 (over x, core).
Axes of the slice: x: 2, y: 2, z: 4, core: 2. Of those that a mesh axis runs over, the one named last changes fastest.
Arguments:
- tokens: bfloat16 [65536, 768], P(('dp', 'ep'))
- out_grad: bfloat16 [65536, 768], P(('dp', 'ep'))
- routes: int32 [65536, 2], P(('dp', 'ep'))
- norm_gain: float32 [768], replicated
- w_router: float32 [768, 8], replicated
- w_gate: bfloat16 [8, 768, 3072], P('ep')
- w_up: bfloat16 [8, 768, 3072], P('ep')
- w_down: bfloat16 [8, 3072, 768], P('ep')
Outputs:
- output 1: bfloat16 [65536, 768], P(('dp', 'ep'))
- output 2: bfloat16 [65536, 768], P(('dp', 'ep'))
- output 3: float32 [768], replicated
- output 4: float32 [768, 8], replicated
- output 5: bfloat16 [8, 768, 3072], P('ep')
- output 6: bfloat16 [8, 768, 3072], P('ep')
- output 7: bfloat16 [8, 3072, 768], P('ep')
All inputs are finite; a program needn't handle non-finite values.
Results may differ from a plain program's by a relative error of at most 0.0136066.
Values are sent between devices in bfloat16 or wider.
A program may use at most 1 GiB of HBM per device.

v0:
```python
import jax
import jax.numpy as jnp
from jax import lax
from jax.sharding import PartitionSpec as P

CAPACITY_NUM = 5
CAPACITY_DEN = 4
NORM_EPS = 1e-5


def slot_maps(route_dev, experts, capacity):
    expert_ids = jnp.arange(experts, dtype=jnp.int32)
    first_hot = (route_dev[..., 0:1] == expert_ids).astype(jnp.int32)
    second_hot = (route_dev[..., 1:2] == expert_ids).astype(jnp.int32)
    first_run = jnp.cumsum(first_hot, axis=-2)
    second_run = jnp.cumsum(second_hot, axis=-2) + first_run[..., -1:, :]
    first_pos = jnp.sum((first_run - 1) * first_hot, axis=-1)
    second_pos = jnp.sum((second_run - 1) * second_hot, axis=-1)
    slot_ids = jnp.arange(experts * capacity, dtype=jnp.int32)
    first_slot = jnp.where(first_pos < capacity, route_dev[..., 0] * capacity + first_pos, -1)
    second_slot = jnp.where(second_pos < capacity, route_dev[..., 1] * capacity + second_pos, -1)
    first_map = (first_slot[..., None] == slot_ids).astype(jnp.bfloat16)
    second_map = (second_slot[..., None] == slot_ids).astype(jnp.bfloat16)
    return first_map, second_map


def solution(mesh):
    ep_size = mesh.shape['ep']
    token_spec = P(('dp', 'ep'), None)
    expert_spec = P('ep', None, None)
    lead_dims = (((0,), (0,)), ((), ()))

    def local_step(tokens, out_grad, routes, norm_gain, w_router, w_gate, w_up, w_down):
        tok_count, model_width = tokens.shape
        local_experts = w_gate.shape[0]
        experts = local_experts * ep_size
        capacity = (CAPACITY_NUM * tok_count * 2 + CAPACITY_DEN * experts - 1) // (CAPACITY_DEN * experts)
        first_map, second_map = slot_maps(routes, experts, capacity)
        both_map = first_map + second_map
        route_hot = (routes[:, :, None] == jnp.arange(experts, dtype=jnp.int32)).astype(jnp.float32)

        x_f32 = tokens.astype(jnp.float32)
        inv_rms = lax.rsqrt(jnp.mean(x_f32 * x_f32, axis=-1, keepdims=True) + NORM_EPS)
        unit_rows = x_f32 * inv_rms
        normed = (unit_rows * norm_gain).astype(jnp.bfloat16)
        logits = jnp.dot(normed, w_router, preferred_element_type=jnp.float32)
        gate_probs = jax.nn.softmax(jnp.einsum('te,tke->tk', logits, route_hot), axis=-1)
        send_rows = lax.dot_general(both_map, normed, lead_dims, preferred_element_type=jnp.float32).astype(jnp.bfloat16)
        recv_rows = lax.all_to_all(send_rows.reshape(ep_size, local_experts, capacity, model_width), 'ep', 0, 1)
        gate_act = jnp.einsum('jscd,jdf->jscf', recv_rows, w_gate, preferred_element_type=jnp.float32)
        up_act = jnp.einsum('jscd,jdf->jscf', recv_rows, w_up, preferred_element_type=jnp.float32)
        silu_gate = jax.nn.silu(gate_act)
        hidden = (silu_gate * up_act).astype(jnp.bfloat16)
        expert_out = jnp.einsum('jscf,jfd->jscd', hidden, w_down, preferred_element_type=jnp.float32).astype(jnp.bfloat16)
        back_rows = lax.all_to_all(expert_out, 'ep', 1, 0).reshape(experts * capacity, model_width)
        first_y = jnp.dot(first_map, back_rows, preferred_element_type=jnp.float32)
        second_y = jnp.dot(second_map, back_rows, preferred_element_type=jnp.float32)
        block_out = (x_f32 + gate_probs[:, 0:1] * first_y + gate_probs[:, 1:2] * second_y).astype(jnp.bfloat16)

        dy_f32 = out_grad.astype(jnp.float32)
        prob_grad = jnp.stack([jnp.sum(dy_f32 * first_y, axis=-1), jnp.sum(dy_f32 * second_y, axis=-1)], axis=-1)
        first_dy = (gate_probs[:, 0:1] * dy_f32).astype(jnp.bfloat16)
        second_dy = (gate_probs[:, 1:2] * dy_f32).astype(jnp.bfloat16)
        d_send = (lax.dot_general(first_map, first_dy, lead_dims, preferred_element_type=jnp.float32) + lax.dot_general(second_map, second_dy, lead_dims, preferred_element_type=jnp.float32)).astype(jnp.bfloat16)
        d_expert_out = lax.all_to_all(d_send.reshape(ep_size, local_experts, capacity, model_width), 'ep', 0, 1)
        d_hidden = jnp.einsum('jscd,jfd->jscf', d_expert_out, w_down, preferred_element_type=jnp.float32)
        grad_down = jnp.einsum('jscf,jscd->jfd', hidden, d_expert_out, preferred_element_type=jnp.float32)
        sig_gate = jax.nn.sigmoid(gate_act)
        d_gate_act = (d_hidden * up_act * sig_gate * (1.0 + gate_act * (1.0 - sig_gate))).astype(jnp.bfloat16)
        d_up_act = (d_hidden * silu_gate).astype(jnp.bfloat16)
        grad_gate = jnp.einsum('jscd,jscf->jdf', recv_rows, d_gate_act, preferred_element_type=jnp.float32)
        grad_up = jnp.einsum('jscd,jscf->jdf', recv_rows, d_up_act, preferred_element_type=jnp.float32)
        d_recv = (jnp.einsum('jscf,jdf->jscd', d_gate_act, w_gate, preferred_element_type=jnp.float32) + jnp.einsum('jscf,jdf->jscd', d_up_act, w_up, preferred_element_type=jnp.float32)).astype(jnp.bfloat16)
        d_back = lax.all_to_all(d_recv, 'ep', 1, 0).reshape(experts * capacity, model_width)
        d_normed = jnp.dot(both_map, d_back, preferred_element_type=jnp.float32)
        d_chosen = gate_probs * (prob_grad - jnp.sum(gate_probs * prob_grad, axis=-1, keepdims=True))
        d_logits = jnp.einsum('tk,tke->te', d_chosen, route_hot)
        d_normed = d_normed + lax.dot_general(d_logits, w_router, (((1,), (1,)), ((), ())))
        grad_router = jnp.einsum('td,te->de', normed, d_logits, preferred_element_type=jnp.float32)
        grad_gain = jnp.sum(d_normed * unit_rows, axis=0)
        d_unit = d_normed * norm_gain
        tokens_grad = (dy_f32 + inv_rms * (d_unit - unit_rows * jnp.mean(d_unit * unit_rows, axis=-1, keepdims=True))).astype(jnp.bfloat16)
        return (block_out, tokens_grad,
                lax.psum(grad_gain, ('dp', 'ep')), lax.psum(grad_router, ('dp', 'ep')),
                lax.psum(grad_gate, 'dp').astype(jnp.bfloat16),
                lax.psum(grad_up, 'dp').astype(jnp.bfloat16),
                lax.psum(grad_down, 'dp').astype(jnp.bfloat16))

    return jax.shard_map(local_step, mesh=mesh,
                         in_specs=(token_spec, token_spec, token_spec, P(None), P(None, None), expert_spec, expert_spec, expert_spec),
                         out_specs=(token_spec, token_spec, P(None), P(None, None), expert_spec, expert_spec, expert_spec),
                         check_vma=False)
```

profile of v0, /device:TPU:14, one launch (start us, length us, event | category | flops | bytes accessed | tf_op | source)
XLA Modules:
  0.0 3038.8 jit_solution(834149010177847049)
XLA Ops:
  0.6 0.0 copy-start
  0.6 0.0 copy-start.8
  0.7 0.0 copy-start.24
  0.7 0.8 fusion.94
  1.5 2.3 reduce-window.14
  3.8 0.3 slice_reduce_fusion.1
  4.1 0.2 reduce-window.15
  4.3 0.1 add_bitcast_fusion.1
  4.4 0.2 slice_reduce_fusion.2
  4.6 2.3 reduce-window.16
  6.9 0.3 slice_reduce_fusion
  7.2 0.2 reduce-window.19
  7.3 0.1 add_bitcast_fusion
  7.5 3.2 copy.95
  10.7 0.0 copy-start.2
  10.7 0.7 fusion.59
  11.4 0.1 fusion.82
  11.5 0.0 copy-done.8
  11.5 34.8 %fusion.40 = bf16[5120,768]{1,0:T(8,128)(2,1)S(1)} fusion(s32[2048]{0:T(1024)S(1)} %bitcast.172, s32[2048]{0:T(1024)S(1)} %bitcast.168, bf16[2048,768]{0,1:T(8,128)(2,1)S(1)} %copy.95, f32[768]{0:T(1024)S(1)} %copy-done.24, f32[2048]{0:T(1024)S(1)} %add_rsqrt_fusion), kind=kOutput, calls=%fused_computation.50 | convolution fusion | flops 16200237056 | bytes 11037696 | tf_op jit(solution)/shard_map/dot_general | solution.py:48
  46.4 90.0 %all_to_all.60 = bf16[4,2,1,640,768]{4,3,1,2,0:T(8,128)(2,1)} all-to-all(bf16[4,2,1,640,768]{4,3,1,2,0:T(8,128)(2,1)S(1)} %bitcast.150), channel_id=1, replica_groups=mesh['dp'=8,'ep'=4] {'ep'}, dimensions={0} | all-to-all | bytes 15728640 | tf_op jit(solution)/shard_map/all_to_all | solution.py:49
  136.4 36.6 %fusion.34 = f32[2,4,640,3072]{3,2,1,0:T(8,128)} fusion(bf16[2,768,3072]{2,1,0:T(8,128)(2,1)} %param.13, bf16[4,2,1,640,768]{4,3,1,2,0:T(8,128)(2,1)} %all_to_all.60), kind=kOutput, calls=%fused_computation.44 | convolution fusion | flops 24159191040 | bytes 80216064 | tf_op jit(solution)/shard_map/jscd,jdf->jscf/dot_general | solution.py:50
  173.0 59.2 %multiply_convert_fusion.2 = (bf16[2,4,640,3072]{3,2,1,0:T(8,128)(2,1)}, f32[2,4,640,3072]{3,2,1,0:T(8,128)}) fusion(f32[2,4,640,3072]{3,2,1,0:T(8,128)} %fusion.34, bf16[2,768,3072]{2,1,0:T(8,128)(2,1)} %param.14, bf16[4,2,1,640,768]{4,3,1,2,0:T(8,128)(2,1)} %all_to_all.60), kind=kOutput, calls=%fused_computation.2 | convolution fusion | flops 24253562880 | bytes 174587904 | tf_op jit(solution)/shard_map/jscd,jdf->jscf/dot_general | solution.py:51
  232.2 30.7 %convert_bitcast_fusion = bf16[1,2,4,640,768]{4,3,2,1,0:T(8,128)(2,1)S(1)} fusion(bf16[2,4,640,3072]{3,2,1,0:T(8,128)(2,1)} %get-tuple-element.70, bf16[2,3072,768]{2,1,0:T(8,128)(2,1)} %param.15), kind=kOutput, calls=%fused_computation.59 | convolution fusion | flops 24163123200 | bytes 48758784 | tf_op jit(solution)/shard_map/jscf,jfd->jscd/dot_general | solution.py:54
  262.9 3.8 copy.98
  266.7 7.8 all-to-all-start.1
  274.5 0.0 copy-start.9
  274.6 4.6 copy.99
  279.2 0.0 copy-done.3
  279.2 0.9 fusion.90
  280.1 0.0 copy-done.9
  280.1 0.1 select_reduce_fusion.1
  280.2 79.9 %all-to-all-done.1 = bf16[1,2,4,640,768]{4,3,1,0,2:T(8,128)(2,1)} async-done(((bf16[1,2,4,640,768]{4,3,1,0,2:T(8,128)(2,1)}), bf16[1,2,4,640,768]{4,3,1,0,2:T(8,128)(2,1)}, u32[]{:S(2)}, u32[]{:S(2)}) %all-to-all-start.1) | async-done | bytes 7864352 | tf_op jit(solution)/shard_map/all_to_all | solution.py:55
  360.1 0.0 copy-done.22
  360.1 22.4 fusion.1
  382.5 23.0 fusion.64
  405.6 0.1 multiply_reduce_fusion
  405.7 22.7 fusion.5
  428.4 0.0 copy-done.15
  428.4 23.0 add_convert_fusion.1
  451.4 7.3 all-to-all-start.2
  458.8 1.6 fusion.87
  460.4 3.6 fusion.95
  464.0 80.3 %all-to-all-done.2 = bf16[4,2,1,640,768]{4,3,1,2,0:T(8,128)(2,1)} async-done(((bf16[4,2,1,640,768]{4,3,1,2,0:T(8,128)(2,1)}), bf16[4,2,1,640,768]{4,3,1,2,0:T(8,128)(2,1)}, u32[]{:S(2)}, u32[]{:S(2)}) %all-to-all-start.2) | async-done | bytes 7864352 | tf_op jit(solution)/shard_map/all_to_all | solution.py:65
  544.3 33.5 %convolution_bitcast_fusion = f32[2,3072,768]{2,1,0:T(8,128)} fusion(bf16[2,4,640,3072]{3,2,1,0:T(8,128)(2,1)} %get-tuple-element.70, bf16[4,2,1,640,768]{4,3,1,2,0:T(8,128)(2,1)} %all-to-all-done.2), kind=kOutput, calls=%fused_computation.51 | convolution fusion | flops 24159191040 | bytes 58195968 | tf_op jit(solution)/shard_map/jscf,jscd->jfd/dot_general | solution.py:67
  577.8 77.7 %multiply_convert_fusion.1 = (bf16[2,4,640,3072]{3,2,1,0:T(8,128)(2,1)}, bf16[2,4,640,3072]{3,2,1,0:T(8,128)(2,1)}) fusion(f32[2,4,640,3072]{3,2,1,0:T(8,128)} %fusion.34, f32[2,4,640,3072]{3,2,1,0:T(8,128)} %get-tuple-element.71, bf16[2,3072,768]{2,1,0:T(8,128)(2,1)} %param.15, bf16[4,2,1,640,768]{4,3,1,2,0:T(8,128)(2,1)} %all-to-all-done.2), kind=kOutput, calls=%fused_computation.1 | convolution fusion | flops 24363663360 | bytes 206045184 | tf_op jit(solution)/shard_map/jscd,jfd->jscf/dot_general | solution.py:66
  655.5 32.6 %fusion.28 = f32[2,4,640,768]{3,2,1,0:T(8,128)} fusion(bf16[2,4,640,3072]{3,2,1,0:T(8,128)(2,1)} %get-tuple-element.61, bf16[2,768,3072]{2,1,0:T(8,128)(2,1)} %param.14), kind=kOutput, calls=%fused_computation.38 | convolution fusion | flops 24159191040 | bytes 56623104 | tf_op jit(solution)/shard_map/jscf,jdf->jscd/dot_general | solution.py:73
  688.1 34.0 %convolution_bitcast_fusion.1 = f32[2,768,3072]{2,1,0:T(8,128)} fusion(bf16[2,4,640,3072]{3,2,1,0:T(8,128)(2,1)} %get-tuple-element.61, bf16[4,2,1,640,768]{4,3,1,2,0:T(8,128)(2,1)} %all_to_all.60), kind=kOutput, calls=%fused_computation.52 | convolution fusion | flops 24159191040 | bytes 58195968 | tf_op jit(solution)/shard_map/jscd,jscf->jdf/dot_general | solution.py:72
  722.1 33.8 %convolution_bitcast_fusion.2 = f32[2,768,3072]{2,1,0:T(8,128)} fusion(bf16[2,4,640,3072]{3,2,1,0:T(8,128)(2,1)} %get-tuple-element.60, bf16[4,2,1,640,768]{4,3,1,2,0:T(8,128)(2,1)} %all_to_all.60), kind=kOutput, calls=%fused_computation.53 | convolution fusion | flops 24159191040 | bytes 58195968 | tf_op jit(solution)/shard_map/jscd,jscf->jdf/dot_general | solution.py:71
  755.8 33.7 %fusion.43 = bf16[1,2,4,640,768]{4,3,2,1,0:T(8,128)(2,1)} fusion(f32[2,4,640,768]{3,2,1,0:T(8,128)} %fusion.28, bf16[2,4,640,3072]{3,2,1,0:T(8,128)(2,1)} %get-tuple-element.60, bf16[2,768,3072]{2,1,0:T(8,128)(2,1)} %param.13), kind=kOutput, calls=%fused_computation.54 | convolution fusion | flops 24167055360 | bytes 64487424 | tf_op jit(solution)/shard_map/jscf,jdf->jscd/dot_general | solution.py:73
  789.5 7.0 copy.102
  796.5 7.1 all-to-all-start.3
  803.6 0.0 copy-start.26
  803.7 2148.4 %all-reduce.3 = (bf16[2,768,3072]{2,1,0:T(8,128)(2,1)}, bf16[2,768,3072]{2,1,0:T(8,128)(2,1)}, bf16[2,3072,768]{2,1,0:T(8,128)(2,1)}) all-reduce(f32[2,768,3072]{2,1,0:T(8,128)} %convolution_bitcast_fusion.2, f32[2,768,3072]{2,1,0:T(8,128)} %convolution_bitcast_fusion.1, ...), channel_id=1, replica_groups=mesh['dp'=8,'ep'=4] {'dp'}, use_global_device_ids=true, to_apply=%region_16.17 | all-reduce | flops 14155776 | bytes 84934656 | tf_op jit(solution)/shard_map/psum | solution.py:85
  2952.1 0.0 all-to-all-done.3
  2952.1 0.0 copy-done.4
  2952.1 0.0 copy-start.6
  2952.1 0.0 copy-start.14
  2952.1 0.0 copy-start.16
  2952.1 24.1 fusion.58
  2976.3 0.0 copy-start.1
  2976.3 8.6 fusion.66
  2984.9 4.8 copy.108
  2989.7 2.8 copy.109
  2992.5 45.9 %all-reduce = (f32[768]{0:T(1024)}, f32[768,8]{0,1:T(8,128)}) all-reduce(f32[768]{0:T(1024)S(1)} %get-tuple-element.49, f32[768,8]{0,1:T(8,128)S(1)} %copy-done.17), channel_id=1, replica_groups=mesh['dp'=8,'ep'=4] {'dp','ep'}, use_global_device_ids=true, to_apply=%region_14.15 | all-reduce | flops 6912 | bytes 55296 | tf_op jit(solution)/shard_map/psum | solution.py:84
  (50 shorter events, 0.3 us)
Async XLA Ops:
  0.6 278.6 %copy-start = (f32[768,8]{0,1:T(8,128)S(1)}, f32[768,8]{0,1:T(8,128)}, u32[]{:S(2)}) copy-start(f32[768,8]{0,1:T(8,128)} %param.12) | copy-start | bytes 73732
  0.6 10.8 copy-start.8
  0.7 10.9 copy-start.24
  10.7 35.7 %copy-start.2 = (bf16[2048,768]{0,1:T(8,128)(2,1)}, bf16[2048,768]{0,1:T(8,128)(2,1)S(1)}, u32[]{:S(2)}) copy-start(bf16[2048,768]{0,1:T(8,128)(2,1)S(1)} %copy.95) | copy-start | bytes 9437188
  11.4 35.0 %copy-start.10 = (f32[2048]{0:T(1024)}, f32[2048]{0:T(1024)S(1)}, u32[]{:S(2)}) copy-start(f32[2048]{0:T(1024)S(1)} %add_rsqrt_fusion) | copy-start | bytes 24580
  11.5 34.9 %copy-start.18 = (s32[2048,1]{0,1:T(1,128)}, s32[2048,1]{0,1:T(1,128)S(1)}, u32[]{:S(2)}) copy-start(s32[2048,1]{0,1:T(1,128)S(1)} %get-tuple-element.66) | copy-start | bytes 24580
  11.5 34.9 %copy-start.21 = (s32[2048,1]{0,1:T(1,128)}, s32[2048,1]{0,1:T(1,128)S(1)}, u32[]{:S(2)}) copy-start(s32[2048,1]{0,1:T(1,128)S(1)} %get-tuple-element.67) | copy-start | bytes 24580
  266.7 12.5 copy-start.3
  266.7 12.5 copy-start.11
  266.7 12.5 copy-start.25
  266.7 93.4 %all-to-all-start.1 = ((bf16[1,2,4,640,768]{4,3,1,0,2:T(8,128)(2,1)}), bf16[1,2,4,640,768]{4,3,1,0,2:T(8,128)(2,1)}, u32[]{:S(2)}, u32[]{:S(2)}) async-start(bf16[1,2,4,640,768]{4,3,1,0,2:T(8,128)(2,1)} %copy.98), calls=%async_computation.1 | async-start | bytes 15728640 | tf_op jit(solution)/shard_map/all_to_all | solution.py:55
  274.5 5.5 copy-start.9
  274.5 85.6 %copy-start.22 = (s32[2048,1]{0,1:T(1,128)S(1)}, s32[2048,1]{0,1:T(1,128)}, u32[]{:S(2)}) copy-start(s32[2048,1]{0,1:T(1,128)} %copy-done.21) | copy-start | bytes 24580
  360.1 22.4 copy-start.5
  360.1 22.4 copy-start.19
  405.6 22.7 copy-start.13
  405.6 22.7 copy-start.15
  451.4 92.9 %all-to-all-start.2 = ((bf16[4,2,1,640,768]{4,3,1,2,0:T(8,128)(2,1)}), bf16[4,2,1,640,768]{4,3,1,2,0:T(8,128)(2,1)}, u32[]{:S(2)}, u32[]{:S(2)}) async-start(bf16[4,2,1,640,768]{4,3,1,2,0:T(8,128)(2,1)} %bitcast.149), calls=%async_computation.2 | async-start | bytes 15728640 | tf_op jit(solution)/shard_map/all_to_all | solution.py:65
  796.5 2155.6 %all-to-all-start.3 = ((bf16[1,2,4,640,768]{4,3,1,0,2:T(8,128)(2,1)}), bf16[1,2,4,640,768]{4,3,1,0,2:T(8,128)(2,1)}, u32[]{:S(2)}, u32[]{:S(2)}) async-start(bf16[1,2,4,640,768]{4,3,1,0,2:T(8,128)(2,1)} %copy.102), calls=%async_computation.3 | async-start | bytes 15728640 | tf_op jit(solution)/shard_map/all_to_all | solution.py:74
  803.6 2148.4 %copy-start.4 = (bf16[2048,768]{0,1:T(8,128)(2,1)S(1)}, bf16[2048,768]{0,1:T(8,128)(2,1)}, u32[]{:S(2)}) copy-start(bf16[2048,768]{0,1:T(8,128)(2,1)} %copy-done.2) | copy-start | bytes 9437188
  803.6 2148.4 %copy-start.12 = (f32[2048]{0:T(1024)S(1)}, f32[2048]{0:T(1024)}, u32[]{:S(2)}) copy-start(f32[2048]{0:T(1024)} %copy-done.10) | copy-start | bytes 24580
  803.6 2148.4 %copy-start.20 = (s32[2048,1]{0,1:T(1,128)S(1)}, s32[2048,1]{0,1:T(1,128)}, u32[]{:S(2)}) copy-start(s32[2048,1]{0,1:T(1,128)} %copy-done.18) | copy-start | bytes 24580
  803.6 2148.5 %copy-start.23 = (s32[2048,1]{0,1:T(1,128)S(1)}, s32[2048,1]{0,1:T(1,128)}, u32[]{:S(2)}) copy-start(s32[2048,1]{0,1:T(1,128)} %copy-done.21) | copy-start | bytes 24580
  803.6 2148.5 %copy-start.26 = (f32[768]{0:T(1024)S(1)}, f32[768]{0:T(1024)}, u32[]{:S(2)}) copy-start(f32[768]{0:T(1024)} %param.11) | copy-start | bytes 9220
  2952.1 24.1 copy-start.6
  2952.1 24.1 copy-start.14
  2952.1 24.1 copy-start.16
  2976.3 62.1 %copy-start.1 = (f32[768,8]{0,1:T(8,128)S(1)}, f32[768,8]{0,1:T(8,128)}, u32[]{:S(2)}) copy-start(f32[768,8]{0,1:T(8,128)} %param.12) | copy-start | bytes 73732
  2984.9 4.8 copy-start.7
  2984.9 7.6 copy-start.17
where the time goes:
time: 3040 us
  blocking collectives  2280 us (75%)
  matrix products  528 us (17%)
  waiting for transfers between devices  160 us (5%)
    psum x1, blocking collectives, local_step(): lax.psum(grad_gate, 'dp').astype(jnp.bfloat16)  2150 us
    all_to_all x1, blocking collectives, local_step(): lax.all_to_all(send_rows.reshape(ep_size, local_experts, capacity, model_...  90 us
    all_to_all x1, waiting for transfers between devices, local_step(): lax.all_to_all(d_send.reshape(ep_size, local_experts, capacity, model_wid...  80.3 us
    all_to_all x1, waiting for transfers between devices, local_step(): lax.all_to_all(expert_out, 'ep', 1, 0)  79.9 us
    dot_general x1, matrix products, local_step(): jnp.einsum('jscd,jfd->jscf', d_expert_out, w_down, preferred_element_type...  77.7 us
  transfers between devices with their start and end apart: 3, of which 2 were waited for; matrix products, arithmetic and copies ran while one was open for 0% of the time, Pallas kernels for 0%

commit v1 on v0

v1 whole, which is shorter than its diff:
```python
import jax
import jax.numpy as jnp
from jax import lax
from jax.sharding import PartitionSpec as P

CAPACITY_NUM = 5
CAPACITY_DEN = 4
NORM_EPS = 1e-5


def slot_ids(route_dev, experts, local_experts, capacity):
    expert_ids = jnp.arange(experts, dtype=jnp.int32)
    first_hot = (route_dev[:, 0:1] == expert_ids).astype(jnp.int32)
    second_hot = (route_dev[:, 1:2] == expert_ids).astype(jnp.int32)
    first_run = jnp.cumsum(first_hot, axis=0)
    second_run = jnp.cumsum(second_hot, axis=0) + first_run[-1:, :]
    first_pos = jnp.sum((first_run - 1) * first_hot, axis=-1)
    second_pos = jnp.sum((second_run - 1) * second_hot, axis=-1)

    def slot(ids, pos):
        rank = (ids % local_experts) * (experts // local_experts) + ids // local_experts
        return jnp.where(pos < capacity, rank * capacity + pos, -1)

    return slot(route_dev[:, 0], first_pos), slot(route_dev[:, 1], second_pos)


def solution(mesh):
    ep_size = mesh.shape['ep']
    token_spec = P(('dp', 'ep'), None)
    expert_spec = P('ep', None, None)
    lead_dims = (((0,), (0,)), ((), ()))
    f32, bf16 = jnp.float32, jnp.bfloat16

    def reduce_over_dp(grad):
        part = lax.psum_scatter(grad, 'dp', scatter_dimension=0, tiled=True)
        return lax.all_gather(part.astype(bf16), 'dp', axis=0, tiled=True)

    def local_step(tokens, out_grad, routes, norm_gain, w_router, w_gate, w_up, w_down):
        tok_count, model_width = tokens.shape
        local_experts = w_gate.shape[0]
        experts = local_experts * ep_size
        capacity = (CAPACITY_NUM * tok_count * 2 + CAPACITY_DEN * experts - 1) // (CAPACITY_DEN * experts)
        held = ep_size * capacity
        first_slot, second_slot = slot_ids(routes, experts, local_experts, capacity)
        route_hot = (routes[:, :, None] == jnp.arange(experts, dtype=jnp.int32)).astype(f32)

        def maps(start, count):
            ids = start + jnp.arange(count, dtype=jnp.int32)
            return (first_slot[:, None] == ids).astype(bf16), (second_slot[:, None] == ids).astype(bf16)

        x_f32 = tokens.astype(f32)
        inv_rms = lax.rsqrt(jnp.mean(x_f32 * x_f32, axis=-1, keepdims=True) + NORM_EPS)
        unit_rows = x_f32 * inv_rms
        normed = (unit_rows * norm_gain).astype(bf16)
        logits = jnp.dot(normed, w_router, preferred_element_type=f32)
        gate_probs = jax.nn.softmax(jnp.einsum('te,tke->tk', logits, route_hot), axis=-1)
        dy_f32 = out_grad.astype(f32)
        first_dy = (gate_probs[:, 0:1] * dy_f32).astype(bf16)
        second_dy = (gate_probs[:, 1:2] * dy_f32).astype(bf16)

        recv, d_out = [], []
        for j in range(local_experts):
            first_map, second_map = maps(j * held, held)
            rows = lax.dot_general(first_map + second_map, normed, lead_dims, preferred_element_type=f32).astype(bf16)
            d_rows = (lax.dot_general(first_map, first_dy, lead_dims, preferred_element_type=f32)
                      + lax.dot_general(second_map, second_dy, lead_dims, preferred_element_type=f32)).astype(bf16)
            recv.append(lax.all_to_all(rows.reshape(ep_size, capacity, model_width), 'ep', 0, 0).reshape(held, model_width))
            d_out.append(lax.all_to_all(d_rows.reshape(ep_size, capacity, model_width), 'ep', 0, 0).reshape(held, model_width))

        saved, grads = [], []
        for j in range(local_experts):
            u, dv = recv[j], d_out[j]
            gate_act = jnp.dot(u, w_gate[j], preferred_element_type=f32)
            up_act = jnp.dot(u, w_up[j], preferred_element_type=f32)
            silu_gate = jax.nn.silu(gate_act)
            hidden = (silu_gate * up_act).astype(bf16)
            grad_down = lax.dot_general(hidden, dv, lead_dims, preferred_element_type=f32)
            d_hidden = lax.dot_general(dv, w_down[j], (((1,), (1,)), ((), ())), preferred_element_type=f32)
            sig_gate = jax.nn.sigmoid(gate_act)
            d_gate_act = (d_hidden * up_act * sig_gate * (1.0 + gate_act * (1.0 - sig_gate))).astype(bf16)
            d_up_act = (d_hidden * silu_gate).astype(bf16)
            grad_gate = lax.dot_general(u, d_gate_act, lead_dims, preferred_element_type=f32)
            grad_up = lax.dot_general(u, d_up_act, lead_dims, preferred_element_type=f32)
            saved.append((hidden, d_gate_act, d_up_act))
            grads.append((grad_down, grad_gate, grad_up))

        reduced = [[reduce_over_dp(g) for g in group] for group in grads]
        saved, _ = lax.optimization_barrier((saved, grads))
        y_rows, d_rows = [], []
        for j in range(local_experts):
            hidden, d_gate_act, d_up_act = saved[j]
            y_rows.append(jnp.dot(hidden, w_down[j], preferred_element_type=f32).astype(bf16))
            trans = (((1,), (1,)), ((), ()))
            d_rows.append((lax.dot_general(d_gate_act, w_gate[j], trans, preferred_element_type=f32)
                           + lax.dot_general(d_up_act, w_up[j], trans, preferred_element_type=f32)).astype(bf16))

        def send_back(rows):
            parts = [lax.all_to_all(r.reshape(ep_size, capacity, model_width), 'ep', 0, 0).reshape(held, model_width) for r in rows]
            return jnp.concatenate(parts, axis=0)

        back_rows = send_back(y_rows)
        d_back = send_back(d_rows)
        first_map, second_map = maps(0, local_experts * held)
        first_y = jnp.dot(first_map, back_rows, preferred_element_type=f32)
        second_y = jnp.dot(second_map, back_rows, preferred_element_type=f32)
        block_out = (x_f32 + gate_probs[:, 0:1] * first_y + gate_probs[:, 1:2] * second_y).astype(bf16)
        prob_grad = jnp.stack([jnp.sum(dy_f32 * first_y, axis=-1), jnp.sum(dy_f32 * second_y, axis=-1)], axis=-1)
        d_chosen = gate_probs * (prob_grad - jnp.sum(gate_probs * prob_grad, axis=-1, keepdims=True))
        d_logits = jnp.einsum('tk,tke->te', d_chosen, route_hot)
        d_normed = jnp.dot(first_map + second_map, d_back, preferred_element_type=f32)
        d_normed = d_normed + lax.dot_general(d_logits, w_router, (((1,), (1,)), ((), ())))
        grad_router = jnp.einsum('td,te->de', normed, d_logits, preferred_element_type=f32)
        grad_gain = jnp.sum(d_normed * unit_rows, axis=0)
        d_unit = d_normed * norm_gain
        tokens_grad = (dy_f32 + inv_rms * (d_unit - unit_rows * jnp.mean(d_unit * unit_rows, axis=-1, keepdims=True))).astype(bf16)

        def stacked(k):
            return jnp.stack([group[k] for group in reduced])

        return (block_out, tokens_grad,
                lax.psum(grad_gain, ('dp', 'ep')), lax.psum(grad_router, ('dp', 'ep')),
                stacked(1), stacked(2), stacked(0))

    return jax.shard_map(local_step, mesh=mesh,
                         in_specs=(token_spec, token_spec, token_spec, P(None), P(None, None), expert_spec, expert_spec, expert_spec),
                         out_specs=(token_spec, token_spec, P(None), P(None, None), expert_spec, expert_spec, expert_spec),
                         check_vma=False)
```

time: 3040 us -> 1710 us (0.56)
  blocking collectives: 2280 us -> 41.8 us
  waiting for transfers between devices: 160 us -> 969 us
  other arithmetic: 14.8 us -> 48.1 us
    psum x1 -> x0, blocking collectives: 2150 us -> none  [local_step(): lax.psum(grad_gate, 'dp').astype(jnp.bfloat16)]
    reduce_scatter x0 -> x6, waiting for transfers between devices: none -> 502 us  [reduce_over_dp(): part = lax.psum_scatter(grad, 'dp', scatter_dimension=0, tiled=True)]
    all_gather x0 -> x6, waiting for transfers between devices: none -> 377 us  [reduce_over_dp(): return lax.all_gather(part.astype(bf16), 'dp', axis=0, tiled=True)]
    all_to_all x1 -> x0, blocking collectives: 90 us -> none  [local_step(): lax.all_to_all(send_rows.reshape(ep_size, local_experts, capacity, model_...]
    all_to_all x3 -> x8, waiting for transfers between devices: 160 us -> 90 us  [the longest x4 44.8 us: send_back(): lax.all_to_all(r.reshape(ep_size, capacity, model_width), 'ep', 0, 0)]
    dot_general x16 -> x27, matrix products: 501 us -> 523 us  [the longest x2 96.2 us: local_step(): lax.dot_general(dv, w_down[j], (((1,), (1,)), ((), ())), preferred_elemen...]
  transfers between devices with their start and end apart: 3 -> 20, of which waited for: 2 -> 16; matrix products, arithmetic and copies ran while one was open for 0% -> 30% of each run, Pallas kernels for 0% -> 0%
where the time goes in v1:
time: 1710 us; the launch traced here: 1690 us
  waiting for transfers between devices  969 us (57%)
  matrix products  548 us (32%)
  starting transfers between devices  49.3 us (3%)
  other arithmetic  48.1 us (3%)
  blocking collectives  41.8 us (2%)
  local copies, waits for them, and re-layouts  21.3 us (1%)
    reduce_scatter x6, waiting for transfers between devices, reduce_over_dp(): part = lax.psum_scatter(grad, 'dp', scatter_dimension=0, tiled=True)  502 us
    all_gather x6, waiting for transfers between devices, reduce_over_dp(): return lax.all_gather(part.astype(bf16), 'dp', axis=0, tiled=True)  377 us
    dot_general x2, matrix products, local_step(): lax.dot_general(dv, w_down[j], (((1,), (1,)), ((), ())), preferred_elemen...  96.2 us
    all_to_all x4, waiting for transfers between devices, send_back(): lax.all_to_all(r.reshape(ep_size, capacity, model_width), 'ep', 0, 0)  44.8 us
    dot_general x2, matrix products, local_step(): gate_act = jnp.dot(u, w_gate[j], preferred_element_type=f32)  42.3 us
    psum x1, blocking collectives, local_step(): lax.psum(grad_gain, ('dp', 'ep'))  41.8 us
    dot_general x2, matrix products, local_step(): lax.dot_general(d_up_act, w_up[j], trans, preferred_element_type=f32)  39.6 us
    dot_general x2, matrix products, local_step(): lax.dot_general(hidden, dv, lead_dims, preferred_element_type=f32)  37.5 us
  transfers between devices with their start and end apart: 20, of which 16 were waited for; matrix products, arithmetic and copies ran while one was open for 30% of the time, Pallas kernels for 0%

profile of v1, /device:TPU:14, one launch (start us, length us, event | category | flops | bytes accessed | tf_op | source)
XLA Modules:
  0.0 1692.8 jit_solution(3310610059749997660)
XLA Ops:
  8.0 2.3 reduce-window.14
  11.0 2.3 reduce-window.16
  14.0 3.2 copy.47
  18.2 12.8 fusion.61
  31.0 5.7 all-to-all-start.2
  36.6 4.6 copy.48
  42.9 11.2 fusion.16
  54.2 11.3 add_convert_fusion.2
  65.5 14.6 all-to-all-done.2
  80.1 6.5 all-to-all-start.3
  86.6 21.1 %fusion.75 = f32[2560,3072]{1,0:T(8,128)} fusion(bf16[2560,768]{1,0:T(8,128)(2,1)} %bitcast.21, bf16[2,768,3072]{2,1,0:T(8,128)(2,1)} %param.13), kind=kOutput, calls=%fused_computation.95 | convolution fusion | flops 12079595520 | bytes 40108032 | tf_op jit(solution)/shard_map/dot_general | solution.py:73
  107.8 18.4 %fusion.71 = f32[2560,3072]{1,0:T(8,128)} fusion(bf16[2560,768]{1,0:T(8,128)(2,1)} %bitcast.21, bf16[2,768,3072]{2,1,0:T(8,128)(2,1)S(1)} %bitcast.186), kind=kOutput, calls=%fused_computation.91 | convolution fusion | flops 12079595520 | bytes 40108032 | tf_op jit(solution)/shard_map/dot_general | solution.py:74
  126.2 4.0 all-to-all-done.3
  130.1 48.1 %multiply_convert_fusion = (bf16[2560,3072]{1,0:T(8,128)(2,1)}, bf16[2560,3072]{1,0:T(8,128)(2,1)}, bf16[2560,3072]{1,0:T(8,128)(2,1)}) fusion(f32[2560,3072]{1,0:T(8,128)} %fusion.75, f32[2560,3072]{1,0:T(8,128)} %fusion.71, bf16[2560,768]{1,0:T(8,128)(2,1)} %bitcast.25, bf16[2,3072,768]{2,1,0:T(8,128)(2,1)} %param.15), kind=kOutput, calls=%fused_computation.6 | convolution fusion | flops 12197560320 | bytes 118751232 | tf_op jit(solution)/shard_map/dot_general | solution.py:78
  178.2 18.9 %fusion.131 = f32[768,3072]{1,0:T(8,128)} fusion(bf16[2560,768]{1,0:T(8,128)(2,1)} %bitcast.21, bf16[2560,3072]{1,0:T(8,128)(2,1)} %get-tuple-element.17), kind=kOutput, calls=%fused_computation.178 | convolution fusion | flops 12079595520 | bytes 29097984 | tf_op jit(solution)/shard_map/dot_general | solution.py:82
  199.0 14.5 fusion.64
  213.4 6.7 all-to-all-start
  220.1 9.4 fusion.19
  229.5 11.5 add_convert_fusion.3
  241.0 22.6 %all-to-all-done = bf16[4,640,768]{2,1,0:T(8,128)(2,1)} async-done(((bf16[4,640,768]{2,1,0:T(8,128)(2,1)}), bf16[4,640,768]{2,1,0:T(8,128)(2,1)}, u32[]{:S(2)}, u32[]{:S(2)}) %all-to-all-start) | async-done | bytes 3932192 | tf_op jit(solution)/shard_map/all_to_all | solution.py:67
  263.6 6.5 all-to-all-start.1
  270.1 21.1 %fusion.85 = f32[2560,3072]{1,0:T(8,128)} fusion(bf16[2560,768]{1,0:T(8,128)(2,1)} %bitcast.13, bf16[2,768,3072]{2,1,0:T(8,128)(2,1)} %param.13), kind=kOutput, calls=%fused_computation.105 | convolution fusion | flops 12079595520 | bytes 40108032 | tf_op jit(solution)/shard_map/dot_general | solution.py:73
  291.3 18.4 %fusion.81 = f32[2560,3072]{1,0:T(8,128)} fusion(bf16[2560,768]{1,0:T(8,128)(2,1)} %bitcast.13, bf16[2,768,3072]{2,1,0:T(8,128)(2,1)S(1)} %bitcast.188), kind=kOutput, calls=%fused_computation.101 | convolution fusion | flops 12079595520 | bytes 40108032 | tf_op jit(solution)/shard_map/dot_general | solution.py:74
  309.6 4.0 all-to-all-done.1
  313.6 48.1 %multiply_convert_fusion.3 = (bf16[2560,3072]{1,0:T(8,128)(2,1)}, bf16[2560,3072]{1,0:T(8,128)(2,1)}, bf16[2560,3072]{1,0:T(8,128)(2,1)}) fusion(f32[2560,3072]{1,0:T(8,128)} %fusion.85, f32[2560,3072]{1,0:T(8,128)} %fusion.81, bf16[2560,768]{1,0:T(8,128)(2,1)} %bitcast.18, bf16[2,3072,768]{2,1,0:T(8,128)(2,1)} %param.15), kind=kOutput, calls=%fused_computation.11 | convolution fusion | flops 12197560320 | bytes 118751232 | tf_op jit(solution)/shard_map/dot_general | solution.py:78
  361.7 18.3 %fusion.128 = f32[768,3072]{1,0:T(8,128)} fusion(bf16[2560,768]{1,0:T(8,128)(2,1)} %bitcast.13, bf16[2560,3072]{1,0:T(8,128)(2,1)} %get-tuple-element.15), kind=kOutput, calls=%fused_computation.175 | convolution fusion | flops 12079595520 | bytes 29097984 | tf_op jit(solution)/shard_map/dot_general | solution.py:82
  380.0 18.4 %fusion.132 = f32[768,3072]{1,0:T(8,128)} fusion(bf16[2560,768]{1,0:T(8,128)(2,1)} %bitcast.21, bf16[2560,3072]{1,0:T(8,128)(2,1)} %get-tuple-element.18), kind=kOutput, calls=%fused_computation.179 | convolution fusion | flops 12079595520 | bytes 29097984 | tf_op jit(solution)/shard_map/dot_general | solution.py:83
  398.5 18.8 %fusion.129 = f32[768,3072]{1,0:T(8,128)} fusion(bf16[2560,768]{1,0:T(8,128)(2,1)} %bitcast.13, bf16[2560,3072]{1,0:T(8,128)(2,1)} %get-tuple-element.16), kind=kOutput, calls=%fused_computation.176 | convolution fusion | flops 12079595520 | bytes 29097984 | tf_op jit(solution)/shard_map/dot_general | solution.py:83
  417.4 18.6 %fusion.130 = f32[3072,768]{1,0:T(8,128)} fusion(bf16[2560,3072]{1,0:T(8,128)(2,1)} %get-tuple-element.14, bf16[2560,768]{1,0:T(8,128)(2,1)} %bitcast.25), kind=kOutput, calls=%fused_computation.177 | convolution fusion | flops 12079595520 | bytes 29097984 | tf_op jit(solution)/shard_map/dot_general | solution.py:77
  436.1 18.9 %fusion.127 = f32[3072,768]{1,0:T(8,128)} fusion(bf16[2560,3072]{1,0:T(8,128)(2,1)} %get-tuple-element.13, bf16[2560,768]{1,0:T(8,128)(2,1)} %bitcast.18), kind=kOutput, calls=%fused_computation.174 | convolution fusion | flops 12079595520 | bytes 29097984 | tf_op jit(solution)/shard_map/dot_general | solution.py:77
  455.1 2.2 convert_element_type.140
  457.4 84.6 %reduce-scatter.7.cloned.1.call-done = f32[96,3072]{1,0:T(8,128)} async-done(((f32[768,3072]{1,0:T(8,128)}), f32[96,3072]{1,0:T(8,128)}) %reduce-scatter.7.cloned.1.call-update) | async-done | bytes 1179664 | tf_op jit(solution)/shard_map/reduce_scatter | solution.py:35
  544.1 162.4 %reduce-scatter.13.cloned.1.call-done = f32[96,3072]{1,0:T(8,128)} async-done(((f32[768,3072]{1,0:T(8,128)}), f32[96,3072]{1,0:T(8,128)}) %reduce-scatter.13.cloned.1.call-update) | async-done | bytes 1179664 | tf_op jit(solution)/shard_map/reduce_scatter | solution.py:35
  708.8 17.7 %convolution_convert_fusion = bf16[2560,768]{1,0:T(8,128)(2,1)} fusion(bf16[2560,3072]{1,0:T(8,128)(2,1)} %get-tuple-element.14, bf16[2,3072,768]{2,1,0:T(8,128)(2,1)} %param.15), kind=kOutput, calls=%fused_computation.85 | convolution fusion | flops 12081561600 | bytes 24379392 | tf_op jit(solution)/shard_map/dot_general | solution.py:92
  726.5 5.3 all-to-all-start.5
  731.8 17.7 %convolution_convert_fusion.1 = bf16[2560,768]{1,0:T(8,128)(2,1)} fusion(bf16[2560,3072]{1,0:T(8,128)(2,1)} %get-tuple-element.13, bf16[2,3072,768]{2,1,0:T(8,128)(2,1)} %param.15), kind=kOutput, calls=%fused_computation.86 | convolution fusion | flops 12081561600 | bytes 24379392 | tf_op jit(solution)/shard_map/dot_general | solution.py:92
  749.5 121.0 %reduce-scatter.11.cloned.1.call-done = f32[96,3072]{1,0:T(8,128)} async-done(((f32[768,3072]{1,0:T(8,128)}), f32[96,3072]{1,0:T(8,128)}) %reduce-scatter.11.cloned.1.call-update) | async-done | bytes 1179664 | tf_op jit(solution)/shard_map/reduce_scatter | solution.py:35
  872.8 19.0 %fusion.73 = f32[2560,768]{1,0:T(8,128)} fusion(bf16[2560,3072]{1,0:T(8,128)(2,1)} %get-tuple-element.17, bf16[2,768,3072]{2,1,0:T(8,128)(2,1)} %param.13), kind=kOutput, calls=%fused_computation.93 | convolution fusion | flops 12079595520 | bytes 28311552 | tf_op jit(solution)/shard_map/dot_general | solution.py:94
  891.7 19.8 %add_convert_fusion = bf16[2560,768]{1,0:T(8,128)(2,1)} fusion(f32[2560,768]{1,0:T(8,128)} %fusion.73, bf16[2560,3072]{1,0:T(8,128)(2,1)} %get-tuple-element.18, bf16[2,768,3072]{2,1,0:T(8,128)(2,1)} %param.14), kind=kOutput, calls=%fused_computation.66 | convolution fusion | flops 12083527680 | bytes 32243712 | tf_op jit(solution)/shard_map/dot_general | solution.py:95
  911.5 17.0 %fusion.83 = f32[2560,768]{1,0:T(8,128)} fusion(bf16[2560,3072]{1,0:T(8,128)(2,1)} %get-tuple-element.15, bf16[2,768,3072]{2,1,0:T(8,128)(2,1)S(1)} %bitcast.184), kind=kOutput, calls=%fused_computation.103 | convolution fusion | flops 12079595520 | bytes 28311552 | tf_op jit(solution)/shard_map/dot_general | solution.py:94
  928.5 106.0 %reduce-scatter.17.cloned.1.call-done = f32[384,768]{1,0:T(8,128)} async-done(((f32[3072,768]{1,0:T(8,128)}), f32[384,768]{1,0:T(8,128)}) %reduce-scatter.17.cloned.1.call-update) | async-done | bytes 1179664 | tf_op jit(solution)/shard_map/reduce_scatter | solution.py:35
  1036.7 5.5 all-to-all-start.4
  1042.2 19.8 %add_convert_fusion.1 = bf16[2560,768]{1,0:T(8,128)(2,1)} fusion(f32[2560,768]{1,0:T(8,128)} %fusion.83, bf16[2560,3072]{1,0:T(8,128)(2,1)} %get-tuple-element.16, bf16[2,768,3072]{2,1,0:T(8,128)(2,1)} %param.14), kind=kOutput, calls=%fused_computation.67 | convolution fusion | flops 12083527680 | bytes 32243712 | tf_op jit(solution)/shard_map/dot_general | solution.py:95
  1062.0 23.6 %all-to-all-done.4 = bf16[4,640,768]{2,1,0:T(8,128)(2,1)} async-done(((bf16[4,640,768]{2,1,0:T(8,128)(2,1)}), bf16[4,640,768]{2,1,0:T(8,128)(2,1)}, u32[]{:S(2)}, u32[]{:S(2)}) %all-to-all-start.4) | async-done | bytes 3932192 | tf_op jit(solution)/shard_map/all_to_all | solution.py:98
  1085.7 6.4 all-to-all-start.7
  1092.1 22.3 %fusion.1 = f32[2048,768]{0,1:T(8,128)} fusion(s32[2048]{0:T(1024)S(1)} %bitcast.175, bf16[2560,768]{1,0:T(8,128)(2,1)} %bitcast.30, bf16[2560,768]{1,0:T(8,128)(2,1)} %bitcast.28), kind=kOutput, calls=%fused_computation.2 | convolution fusion | flops 16132341760 | bytes 14163968 | tf_op jit(solution)/shard_map/dot_general | solution.py:105
  1114.4 21.2 %all-to-all-done.7 = bf16[4,640,768]{2,1,0:T(8,128)(2,1)} async-done(((bf16[4,640,768]{2,1,0:T(8,128)(2,1)}), bf16[4,640,768]{2,1,0:T(8,128)(2,1)}, u32[]{:S(2)}, u32[]{:S(2)}) %all-to-all-start.7) | async-done | bytes 3932192 | tf_op jit(solution)/shard_map/all_to_all | solution.py:98
  1135.6 6.4 all-to-all-start.6
  1142.0 24.2 %fusion.56 = (f32[2048]{0:T(1024)S(1)}, f32[2048]{0:T(1024)S(1)}, bf16[2048,768]{0,1:T(8,128)(2,1)}) fusion(bf16[2048,768]{0,1:T(8,128)(2,1)} %copy.48, f32[2048,768]{0,1:T(8,128)} %fusion.1, f32[2048]{0:T(1024)S(1)} %bitcast.182, f32[2048]{0:T(1024)S(1)} %bitcast.179, bf16[2048,768]{0,1:T(8,128)(2,1)S(1)} %copy-done.3, bf16[2560,768]{1,0:T(8,128)(2,1)} %bitcast.30, ...), kind=kOutput, calls=%fused_computation.80 | convolution fusion | flops 16149639168 | bytes 23633920 | tf_op jit(solution)/shard_map/dot_general | solution.py:104
  1166.2 4.7 copy.51
  1170.8 27.6 %reduce-scatter.15.cloned.1.call-done = f32[384,768]{1,0:T(8,128)} async-done(((f32[3072,768]{1,0:T(8,128)}), f32[384,768]{1,0:T(8,128)}) %reduce-scatter.15.cloned.1.call-update) | async-done | bytes 1179664 | tf_op jit(solution)/shard_map/reduce_scatter | solution.py:35
  1200.8 27.0 %fusion.7 = f32[2048,768]{0,1:T(8,128)} fusion(s32[2048]{0:T(1024)S(1)} %bitcast.176, s32[2048]{0:T(1024)S(1)} %bitcast.170, bf16[2560,768]{1,0:T(8,128)(2,1)} %bitcast.34, bf16[2560,768]{1,0:T(8,128)(2,1)} %bitcast.32), kind=kOutput, calls=%fused_computation.17 | convolution fusion | flops 16205742080 | bytes 14172160 | tf_op jit(solution)/shard_map/dot_general | solution.py:110
  1227.8 4.4 fusion.50
  1232.3 3.7 fusion.58
  1236.0 4.6 copy.52
  1241.6 41.8 %all-reduce = (f32[768]{0:T(1024)}, f32[768,8]{0,1:T(8,128)}) all-reduce(f32[768]{0:T(1024)S(1)} %get-tuple-element.54, f32[768,8]{0,1:T(8,128)S(1)} %fusion.119), channel_id=1, replica_groups=mesh['dp'=8,'ep'=4] {'dp','ep'}, use_global_device_ids=true, to_apply=%region_14.15 | all-reduce | flops 6912 | bytes 55296 | tf_op jit(solution)/shard_map/psum | solution.py:121
  1283.4 75.3 %all-gather.7.cloned.1.call-done = bf16[768,3072]{1,0:T(8,128)(2,1)} async-done(((bf16[96,3072]{1,0:T(8,128)(2,1)}), bf16[768,3072]{1,0:T(8,128)(2,1)}) %all-gather.7.cloned.1.call-update) | async-done | bytes 4718608 | tf_op jit(solution)/shard_map/all_gather | solution.py:36
  1358.6 8.4 pad_maximum_fusion
  1367.0 71.3 %all-gather.13.cloned.1.call-done = bf16[768,3072]{1,0:T(8,128)(2,1)} async-done(((bf16[96,3072]{1,0:T(8,128)(2,1)}), bf16[768,3072]{1,0:T(8,128)(2,1)}) %all-gather.13.cloned.1.call-update) | async-done | bytes 4718608 | tf_op jit(solution)/shard_map/all_gather | solution.py:36
  1438.3 79.5 %all-gather.11.cloned.1.call-done = bf16[768,3072]{1,0:T(8,128)(2,1)} async-done(((bf16[96,3072]{1,0:T(8,128)(2,1)}), bf16[768,3072]{1,0:T(8,128)(2,1)}) %all-gather.11.cloned.1.call-update) | async-done | bytes 4718608 | tf_op jit(solution)/shard_map/all_gather | solution.py:36
  1517.9 8.4 pad_maximum_fusion.1
  1526.3 71.3 %all-gather.17.cloned.1.call-done = bf16[3072,768]{1,0:T(8,128)(2,1)} async-done(((bf16[384,768]{1,0:T(8,128)(2,1)}), bf16[3072,768]{1,0:T(8,128)(2,1)}) %all-gather.17.cloned.1.call-update) | async-done | bytes 4718608 | tf_op jit(solution)/shard_map/all_gather | solution.py:36
  1597.6 79.5 %all-gather.15.cloned.1.call-done = bf16[3072,768]{1,0:T(8,128)(2,1)} async-done(((bf16[384,768]{1,0:T(8,128)(2,1)}), bf16[3072,768]{1,0:T(8,128)(2,1)}) %all-gather.15.cloned.1.call-update) | async-done | bytes 4718608 | tf_op jit(solution)/shard_map/all_gather | solution.py:36
  1677.1 8.4 pad_maximum_fusion.2
  (146 shorter events, 19.1 us)
Async XLA Ops:
  7.2 34.1 %copy-start = (f32[768,8]{0,1:T(8,128)S(1)}, f32[768,8]{0,1:T(8,128)}, u32[]{:S(2)}) copy-start(f32[768,8]{0,1:T(8,128)} %param.12) | copy-start | bytes 73732
  7.2 10.8 copy-start.9
  7.2 11.0 copy-start.18
  17.2 24.1 %copy-start.1 = (bf16[2048,768]{0,1:T(8,128)(2,1)}, bf16[2048,768]{0,1:T(8,128)(2,1)S(1)}, u32[]{:S(2)}) copy-start(bf16[2048,768]{0,1:T(8,128)(2,1)S(1)} %copy.47) | copy-start | bytes 9437188
  17.9 23.4 %copy-start.15 = (f32[2048]{0:T(1024)}, f32[2048]{0:T(1024)S(1)}, u32[]{:S(2)}) copy-start(f32[2048]{0:T(1024)S(1)} %add_rsqrt_fusion) | copy-start | bytes 24580
  18.2 24.8 %copy-start.21 = (s32[2048,1]{0,1:T(1,128)}, s32[2048,1]{0,1:T(1,128)S(1)}, u32[]{:S(2)}) copy-start(s32[2048,1]{0,1:T(1,128)S(1)} %get-tuple-element.69) | copy-start | bytes 24580
  18.2 201.9 %copy-start.24 = (s32[2048,1]{0,1:T(1,128)}, s32[2048,1]{0,1:T(1,128)S(1)}, u32[]{:S(2)}) copy-start(s32[2048,1]{0,1:T(1,128)S(1)} %get-tuple-element.70) | copy-start | bytes 24580
  31.0 49.1 %all-to-all-start.2 = ((bf16[4,640,768]{2,1,0:T(8,128)(2,1)}), bf16[4,640,768]{2,1,0:T(8,128)(2,1)}, u32[]{:S(2)}, u32[]{:S(2)}) async-start(bf16[4,640,768]{2,1,0:T(8,128)(2,1)} %bitcast.148), calls=%async_computation.2 | async-start | bytes 7864320 | tf_op jit(solution)/shard_map/all_to_all | solution.py:67
  42.2 12.0 copy-start.7
  42.3 11.9 copy-start.11
  42.3 0.6 copy-start.13
  42.4 11.8 copy-start.26
  42.4 11.8 copy-start.29
  42.9 11.3 copy-start.4
  80.1 27.7 %slice-start.3 = ((s8[9437184]{0:T(1024)(128)(4,1)}), s8[1048576]{0:T(1024)(128)(4,1)S(1)}, s32[]{:S(2)}) async-start(s8[9437184]{0:T(1024)(128)(4,1)} %bitcast.185), calls=%async_computation.29 | async-start | bytes 2097152
  80.1 50.0 %all-to-all-start.3 = ((bf16[4,640,768]{2,1,0:T(8,128)(2,1)}), bf16[4,640,768]{2,1,0:T(8,128)(2,1)}, u32[]{:S(2)}, u32[]{:S(2)}) async-start(bf16[4,640,768]{2,1,0:T(8,128)(2,1)} %bitcast.149), calls=%async_computation.3 | async-start | bytes 7864320 | tf_op jit(solution)/shard_map/all_to_all | solution.py:68
  86.6 368.5 %reduce-scatter.9.cloned.1.call-start = ((), (), s32[]{:S(2)}) async-start(), calls=%async_computation.16 | async-start | bytes 10616832 | tf_op jit(solution)/shard_map/reduce_scatter | solution.py:35
  86.6 21.2 %slice-start.4 = ((s8[9437184]{0:T(1024)(128)(4,1)}), s8[4194304]{0:T(1024)(128)(4,1)S(1)}, s32[]{:S(2)}) async-start(s8[9437184]{0:T(1024)(128)(4,1)} %bitcast.185), calls=%async_computation.30 | async-start | bytes 8388608
  86.6 21.2 %slice-start.5 = ((s8[9437184]{0:T(1024)(128)(4,1)}), s8[4194304]{0:T(1024)(128)(4,1)S(1)}, s32[]{:S(2)}) async-start(s8[9437184]{0:T(1024)(128)(4,1)} %bitcast.185), calls=%async_computation.31 | async-start | bytes 8388608
  197.1 1.9 copy-start.2
  197.1 1.9 copy-start.16
  197.1 1.9 copy-start.19
  197.1 1.9 copy-start.22
  213.4 6.7 copy-start.5
  213.4 6.7 copy-start.30
  213.4 50.1 %all-to-all-start = ((bf16[4,640,768]{2,1,0:T(8,128)(2,1)}), bf16[4,640,768]{2,1,0:T(8,128)(2,1)}, u32[]{:S(2)}, u32[]{:S(2)}) async-start(bf16[4,640,768]{2,1,0:T(8,128)(2,1)} %bitcast.151), calls=%async_computation | async-start | bytes 7864320 | tf_op jit(solution)/shard_map/all_to_all | solution.py:67
  220.1 9.4 copy-start.27
  263.6 27.7 %slice-start.6 = ((s8[9437184]{0:T(1024)(128)(4,1)}), s8[1048576]{0:T(1024)(128)(4,1)S(1)}, s32[]{:S(2)}) async-start(s8[9437184]{0:T(1024)(128)(4,1)} %bitcast.187), calls=%async_computation.32 | async-start | bytes 2097152
  263.6 50.0 %all-to-all-start.1 = ((bf16[4,640,768]{2,1,0:T(8,128)(2,1)}), bf16[4,640,768]{2,1,0:T(8,128)(2,1)}, u32[]{:S(2)}, u32[]{:S(2)}) async-start(bf16[4,640,768]{2,1,0:T(8,128)(2,1)} %bitcast.150), calls=%async_computation.1 | async-start | bytes 7864320 | tf_op jit(solution)/shard_map/all_to_all | solution.py:68
  270.1 271.8 %reduce-scatter.7.cloned.1.call-start = ((), (), s32[]{:S(2)}) async-start(), calls=%async_computation.14 | async-start | bytes 10616832 | tf_op jit(solution)/shard_map/reduce_scatter | solution.py:35
  270.1 21.1 %slice-start.7 = ((s8[9437184]{0:T(1024)(128)(4,1)}), s8[4194304]{0:T(1024)(128)(4,1)S(1)}, s32[]{:S(2)}) async-start(s8[9437184]{0:T(1024)(128)(4,1)} %bitcast.187), calls=%async_computation.33 | async-start | bytes 8388608
  270.1 21.1 %slice-start.8 = ((s8[9437184]{0:T(1024)(128)(4,1)}), s8[4194304]{0:T(1024)(128)(4,1)S(1)}, s32[]{:S(2)}) async-start(s8[9437184]{0:T(1024)(128)(4,1)} %bitcast.187), calls=%async_computation.34 | async-start | bytes 8388608
  380.0 326.6 %reduce-scatter.13.cloned.1.call-start = ((), (), s32[]{:S(2)}) async-start(), calls=%async_computation.20 | async-start | bytes 10616832 | tf_op jit(solution)/shard_map/reduce_scatter | solution.py:35
  398.5 472.0 %reduce-scatter.11.cloned.1.call-start = ((), (), s32[]{:S(2)}) async-start(), calls=%async_computation.18 | async-start | bytes 10616832 | tf_op jit(solution)/shard_map/reduce_scatter | solution.py:35
  417.3 617.1 %reduce-scatter.17.cloned.1.call-start = ((), (), s32[]{:S(2)}) async-start(), calls=%async_computation.24 | async-start | bytes 10616832 | tf_op jit(solution)/shard_map/reduce_scatter | solution.py:35
  436.1 762.4 %reduce-scatter.15.cloned.1.call-start = ((), (), s32[]{:S(2)}) async-start(), calls=%async_computation.22 | async-start | bytes 10616832 | tf_op jit(solution)/shard_map/reduce_scatter | solution.py:35
  455.0 828.3 %all-gather.9.cloned.1.call-start = ((), (), s32[]{:S(2)}) async-start(), calls=%async_computation.17 | async-start | bytes 5308416 | tf_op jit(solution)/shard_map/all_gather | solution.py:36
  457.3 901.3 %all-gather.7.cloned.1.call-start = ((), (), s32[]{:S(2)}) async-start(), calls=%async_computation.15 | async-start | bytes 5308416 | tf_op jit(solution)/shard_map/all_gather | solution.py:36
  544.1 894.2 %all-gather.13.cloned.1.call-start = ((), (), s32[]{:S(2)}) async-start(), calls=%async_computation.21 | async-start | bytes 5308416 | tf_op jit(solution)/shard_map/all_gather | solution.py:36
  726.5 310.1 %all-to-all-start.5 = ((bf16[4,640,768]{2,1,0:T(8,128)(2,1)}), bf16[4,640,768]{2,1,0:T(8,128)(2,1)}, u32[]{:S(2)}, u32[]{:S(2)}) async-start(bf16[4,640,768]{2,1,0:T(8,128)(2,1)} %bitcast.146), calls=%async_computation.5 | async-start | bytes 7864320 | tf_op jit(solution)/shard_map/all_to_all | solution.py:98
  731.8 786.0 %all-gather.11.cloned.1.call-start = ((), (), s32[]{:S(2)}) async-start(), calls=%async_computation.19 | async-start | bytes 5308416 | tf_op jit(solution)/shard_map/all_gather | solution.py:36
  872.7 724.9 %all-gather.17.cloned.1.call-start = ((), (), s32[]{:S(2)}) async-start(), calls=%async_computation.25 | async-start | bytes 5308416 | tf_op jit(solution)/shard_map/all_gather | solution.py:36
  872.7 38.7 %slice-start = ((s8[9437184]{0:T(1024)(128)(4,1)}), s8[4194304]{0:T(1024)(128)(4,1)S(1)}, s32[]{:S(2)}) async-start(s8[9437184]{0:T(1024)(128)(4,1)} %bitcast.183), calls=%async_computation.26 | async-start | bytes 8388608
  872.8 38.7 %slice-start.1 = ((s8[9437184]{0:T(1024)(128)(4,1)}), s8[4194304]{0:T(1024)(128)(4,1)S(1)}, s32[]{:S(2)}) async-start(s8[9437184]{0:T(1024)(128)(4,1)} %bitcast.183), calls=%async_computation.27 | async-start | bytes 8388608
  891.7 19.8 %slice-start.2 = ((s8[9437184]{0:T(1024)(128)(4,1)}), s8[1048576]{0:T(1024)(128)(4,1)S(1)}, s32[]{:S(2)}) async-start(s8[9437184]{0:T(1024)(128)(4,1)} %bitcast.183), calls=%async_computation.28 | async-start | bytes 2097152
  1036.7 49.0 %all-to-all-start.4 = ((bf16[4,640,768]{2,1,0:T(8,128)(2,1)}), bf16[4,640,768]{2,1,0:T(8,128)(2,1)}, u32[]{:S(2)}, u32[]{:S(2)}) async-start(bf16[4,640,768]{2,1,0:T(8,128)(2,1)} %bitcast.145), calls=%async_computation.4 | async-start | bytes 7864320 | tf_op jit(solution)/shard_map/all_to_all | solution.py:98
  1062.0 30.1 %copy-start.25 = (s32[2048,1]{0,1:T(1,128)S(1)}, s32[2048,1]{0,1:T(1,128)}, u32[]{:S(2)}) copy-start(s32[2048,1]{0,1:T(1,128)} %copy-done.24) | copy-start | bytes 24580
  1085.7 49.9 %all-to-all-start.7 = ((bf16[4,640,768]{2,1,0:T(8,128)(2,1)}), bf16[4,640,768]{2,1,0:T(8,128)(2,1)}, u32[]{:S(2)}, u32[]{:S(2)}) async-start(bf16[4,640,768]{2,1,0:T(8,128)(2,1)} %bitcast.147), calls=%async_computation.7 | async-start | bytes 7864320 | tf_op jit(solution)/shard_map/all_to_all | solution.py:98
  1114.4 27.6 %copy-start.3 = (bf16[2048,768]{0,1:T(8,128)(2,1)S(1)}, bf16[2048,768]{0,1:T(8,128)(2,1)}, u32[]{:S(2)}) copy-start(bf16[2048,768]{0,1:T(8,128)(2,1)} %copy-done.1) | copy-start | bytes 9437188
  1114.4 27.6 %copy-start.23 = (s32[2048,1]{0,1:T(1,128)S(1)}, s32[2048,1]{0,1:T(1,128)}, u32[]{:S(2)}) copy-start(s32[2048,1]{0,1:T(1,128)} %copy-done.21) | copy-start | bytes 24580
  1114.4 27.6 %copy-start.28 = (f32[2048,1]{0,1:T(1,128)S(1)}, f32[2048,1]{0,1:T(1,128)}, u32[]{:S(2)}) copy-start(f32[2048,1]{0,1:T(1,128)} %copy-done.26) | copy-start | bytes 24580
  1114.4 27.6 %copy-start.31 = (f32[2048,1]{0,1:T(1,128)S(1)}, f32[2048,1]{0,1:T(1,128)}, u32[]{:S(2)}) copy-start(f32[2048,1]{0,1:T(1,128)} %copy-done.29) | copy-start | bytes 24580
  1135.6 65.2 %all-to-all-start.6 = ((bf16[4,640,768]{2,1,0:T(8,128)(2,1)}), bf16[4,640,768]{2,1,0:T(8,128)(2,1)}, u32[]{:S(2)}, u32[]{:S(2)}) async-start(bf16[4,640,768]{2,1,0:T(8,128)(2,1)} %bitcast.144), calls=%async_computation.6 | async-start | bytes 7864320 | tf_op jit(solution)/shard_map/all_to_all | solution.py:98
  1142.0 535.2 %all-gather.15.cloned.1.call-start = ((), (), s32[]{:S(2)}) async-start(), calls=%async_computation.23 | async-start | bytes 5308416 | tf_op jit(solution)/shard_map/all_gather | solution.py:36
  1166.1 34.4 %copy-start.8 = (f32[2048,2]{0,1:T(2,128)S(1)}, f32[2048,2]{0,1:T(2,128)}, u32[]{:S(2)}) copy-start(f32[2048,2]{0,1:T(2,128)} %copy-done.7) | copy-start | bytes 49156
  1166.1 34.4 %copy-start.12 = (f32[2048]{0:T(1024)S(1)}, f32[2048]{0:T(1024)}, u32[]{:S(2)}) copy-start(f32[2048]{0:T(1024)} %copy-done.11) | copy-start | bytes 24580
  1166.1 34.4 %copy-start.14 = (f32[2048]{0:T(1024)S(1)}, f32[2048]{0:T(1024)}, u32[]{:S(2)}) copy-start(f32[2048]{0:T(1024)} %copy-done.13) | copy-start | bytes 24580
  1166.1 34.6 %copy-start.10 = (s32[2048,2]{0,1:T(2,128)S(1)}, s32[2048,2]{0,1:T(2,128)}, u32[]{:S(2)}) copy-start(s32[2048,2]{0,1:T(2,128)} %param.10) | copy-start | bytes 49156
  1200.8 27.1 %copy-start.17 = (f32[2048]{0:T(1024)S(1)}, f32[2048]{0:T(1024)}, u32[]{:S(2)}) copy-start(f32[2048]{0:T(1024)} %copy-done.15) | copy-start | bytes 24580
  1200.8 27.1 %copy-start.20 = (f32[768]{0:T(1024)S(1)}, f32[768]{0:T(1024)}, u32[]{:S(2)}) copy-start(f32[768]{0:T(1024)} %param.11) | copy-start | bytes 9220
  1227.8 4.5 copy-start.6
Sparse Core Ops, SparseCore 0:
  197.2 161.7 reduce-scatter.8
  380.1 161.7 reduce-scatter.6
  546.1 160.4 reduce-scatter.12
  710.0 160.4 reduce-scatter.10
  874.0 160.4 reduce-scatter.16
  1037.9 160.4 reduce-scatter.14
  1200.6 78.4 all-gather.8
  1281.3 77.3 all-gather.6
  1360.8 77.4 all-gather.12
  1440.4 77.4 all-gather.10
  1520.1 77.4 all-gather.16
  1599.6 77.4 all-gather.14
